TPU v7x, 32 devices: a whole 2x2x4 slice. The times are simulated.
32 devices in a mesh: row: 8 (over z, x), col: 4 (over y, core).
Axes of the slice: x: 2, y: 2, z: 4, core: 2. Of those that a mesh axis runs over, the one named last changes fastest.
Arguments:
- frontier: bfloat16 [8192, 128], P(('row', 'col')), may hold values from 0 to 8, as said below
- visited: int32 [8192, 128], P(('row', 'col')), may hold values 0 or 1
- tile_rows: int32 [8, 4, 8, 20], P('row', 'col'), may hold values from 0 to 1
- tile_cols: int32 [8, 4, 8, 20], P('row', 'col'), may hold values from 0 to 7
- tile_bits: bfloat16 [8, 4, 8, 20, 128, 128], P('row', 'col'), may hold values from 0 to 1, as said below
Outputs:
- depth_out: int32 [8192, 128], P(('row', 'col'))
- reach_out: float32 [8192, 128], P(('row', 'col'))
Inputs may be any that keep to these rules, and one draw needn't show every extreme that they name: `frontier`: every entry is 0 or lies between 0.25 and 8. `tile_bits`: entries are 0 or 1.
All inputs are finite; a program needn't handle non-finite values. No bound on the sum of `visited` on one device may be relied on, other than what follows from the above.
Results may differ from a plain program's by a relative error of at most 0.0065.
Values may be sent and summed in bfloat16 or wider, within the bound.
A program may use at most 64 MiB of HBM per device.

v0:
```python
import jax
import jax.numpy as jnp
from jax import lax
from jax.sharding import PartitionSpec as P

LEVELS = 4


def on_device(frontier, visited, tile_rows, tile_cols, tile_bits):
    row_index = tile_rows[0, 0]
    col_index = tile_cols[0, 0]
    tile_data = tile_bits[0, 0]
    per_dev, sources = frontier.shape
    tile_size = tile_data.shape[-1]
    col_tiles = lax.axis_size("col") * per_dev // tile_size
    col_onehot = (
        col_index[:, :, None] == jnp.arange(col_tiles, dtype=jnp.int32)[None, None, :]
    ).astype(jnp.float32)
    visited_now = (visited != 0) | (frontier > 0)
    depth_out = jnp.where(visited_now, 0, LEVELS + 1).astype(jnp.int32)
    reach_out = frontier.astype(jnp.float32)
    scaling = jnp.ones((sources,), jnp.float32)
    current = frontier
    for level_step in range(1, LEVELS + 1):
        gathered = lax.all_gather(current, "row", axis=0, tiled=True)
        shard_count = gathered.shape[0] // per_dev
        blocked = gathered.reshape(shard_count, per_dev // tile_size, tile_size, sources)
        picked = jnp.take_along_axis(blocked, row_index[:, :, None, None], axis=1)
        products = jnp.einsum(
            "qtkn,qtks->qtns", tile_data, picked, preferred_element_type=jnp.float32
        )
        partial_value = jnp.einsum(
            "qtm,qtns->mns",
            col_onehot,
            products,
            precision=lax.Precision.HIGHEST,
            preferred_element_type=jnp.float32,
        )
        raw_sum = lax.psum_scatter(
            partial_value.reshape(-1, sources).astype(jnp.bfloat16),
            "col",
            scatter_dimension=0,
            tiled=True,
        ).astype(jnp.float32)
        newly_hit = (raw_sum > 0) & jnp.logical_not(visited_now)
        reached = jnp.where(newly_hit, raw_sum, jnp.zeros_like(raw_sum))
        counted = jnp.sum(newly_hit.astype(jnp.float32), axis=0)
        totals = jnp.sum(reached, axis=0)
        counted, totals = lax.psum((counted, totals), ("row", "col"))
        scaling = scaling / jnp.maximum(scaling * totals / jnp.maximum(counted, 1.0), 1.0)
        reach_out = reach_out + scaling[None, :] * reached
        depth_out = jnp.where(newly_hit, level_step, depth_out)
        visited_now = visited_now | newly_hit
        current = reached.astype(jnp.bfloat16)
    return (depth_out, reach_out)


def solution(mesh):
    placed = (
        P(("row", "col"), None),
        P(("row", "col"), None),
        P("row", "col", None, None),
        P("row", "col", None, None),
        P("row", "col", None, None, None, None),
    )
    return jax.shard_map(
        on_device,
        mesh=mesh,
        in_specs=placed,
        out_specs=(P(("row", "col"), None), P(("row", "col"), None)),
        check_vma=False,
    )
```

profile of v0, /device:TPU:0, one launch (start us, length us, event | category | flops | bytes accessed | tf_op | source)
XLA Modules:
  0.0 445.9 jit_solution(860876956006624836)
XLA Ops:
  8.7 33.2 %all_gather.12 = bf16[2048,128]{1,0:T(8,128)(2,1)S(1)} all-gather(bf16[256,128]{1,0:T(8,128)(2,1)} %param.7), channel_id=1, replica_groups=mesh['row'=8,'col'=4] {'row'}, dimensions={0}, use_global_device_ids=true | all-gather | bytes 589824 | tf_op jit(solution)/shard_map/all_gather | solution.py:25
  41.9 12.2 %gather_fusion = bf16[160,128,128]{2,1,0:T(8,128)(2,1)} fusion(bf16[8,2,128,128]{3,2,1,0:T(8,128)(2,1)S(1)} %bitcast.97, s32[160]{0:T(256)S(1)} %reshape.99), kind=kCustom, calls=%fused_computation.clone | custom fusion | bytes 10487040 | tf_op jit(solution)/shard_map/jit(take_along_axis)/gather | solution.py:28
  54.1 10.0 %fusion.14 = f32[8,20,128,128]{3,2,1,0:T(8,128)} fusion(bf16[1,1,8,20,128,128]{5,4,3,2,1,0:T(8,128)(2,1)} %param.11, bf16[8,20,128,128]{3,2,1,0:T(8,128)(2,1)} %bitcast.99, pred[8,20]{1,0:T(8,128)(4,1)S(1)} %and_bitcast_fusion), kind=kOutput, calls=%fused_computation.18 | convolution fusion | flops 673710080 | bytes 20971680 | tf_op jit(solution)/shard_map/qtkn,qtks->qtns/dot_general | solution.py:29
  64.1 11.9 %copy.11 = f32[8,20,128,128]{2,1,0,3:T(8,128)} copy(f32[8,20,128,128]{3,2,1,0:T(8,128)} %fusion.14) | data formatting | bytes 20971520 | tf_op jit(solution)/shard_map/qtkn,qtks->qtns/dot_general | solution.py:29
  76.0 8.2 %fusion.49 = bf16[8,128,128]{2,0,1:T(8,128)(2,1)S(1)} fusion(f32[8,20,128,128]{2,1,0,3:T(8,128)} %copy.11, s32[8,20]{1,0:T(8,128)S(1)} %bitcast.106), kind=kOutput, calls=%fused_computation.39 | convolution fusion | flops 251790592 | bytes 10748544 | tf_op jit(solution)/shard_map/qtm,qtns->mns/dot_general | solution.py:32
  85.0 21.2 %reduce-scatter.5.cloned.1.call-done = bf16[256,128]{1,0:T(8,128)(2,1)} async-done(((bf16[1024,128]{1,0:T(8,128)(2,1)}), bf16[256,128]{1,0:T(8,128)(2,1)}) %reduce-scatter.5.cloned.1.call-update) | async-done | bytes 65552 | tf_op jit(solution)/shard_map/reduce_scatter | solution.py:39
  108.0 31.8 %all_gather.13 = bf16[2048,128]{1,0:T(8,128)(2,1)S(1)} all-gather(bf16[256,128]{1,0:T(8,128)(2,1)S(1)} %fusion.54), channel_id=1, replica_groups=mesh['row'=8,'col'=4] {'row'}, dimensions={0}, use_global_device_ids=true | all-gather | bytes 589824 | tf_op jit(solution)/shard_map/all_gather | solution.py:25
  139.8 12.2 %gather_fusion.1 = bf16[160,128,128]{2,1,0:T(8,128)(2,1)} fusion(bf16[8,2,128,128]{3,2,1,0:T(8,128)(2,1)S(1)} %bitcast.95, s32[160]{0:T(256)S(1)} %reshape.99), kind=kCustom, calls=%fused_computation.1.clone | custom fusion | bytes 10487040 | tf_op jit(solution)/shard_map/jit(take_along_axis)/gather | solution.py:28
  152.0 10.0 %fusion.12 = f32[8,20,128,128]{3,2,1,0:T(8,128)} fusion(bf16[1,1,8,20,128,128]{5,4,3,2,1,0:T(8,128)(2,1)} %param.11, bf16[8,20,128,128]{3,2,1,0:T(8,128)(2,1)} %bitcast.100, pred[8,20]{1,0:T(8,128)(4,1)S(1)} %and_bitcast_fusion), kind=kOutput, calls=%fused_computation.16 | convolution fusion | flops 673710080 | bytes 20971680 | tf_op jit(solution)/shard_map/qtkn,qtks->qtns/dot_general | solution.py:29
  162.0 11.9 %copy.13 = f32[8,20,128,128]{2,1,0,3:T(8,128)} copy(f32[8,20,128,128]{3,2,1,0:T(8,128)} %fusion.12) | data formatting | bytes 20971520 | tf_op jit(solution)/shard_map/qtkn,qtks->qtns/dot_general | solution.py:29
  173.9 8.1 %fusion.46 = bf16[8,128,128]{2,0,1:T(8,128)(2,1)S(1)} fusion(f32[8,20,128,128]{2,1,0,3:T(8,128)} %copy.13, s32[8,20]{1,0:T(8,128)S(1)} %bitcast.107), kind=kOutput, calls=%fused_computation.38 | convolution fusion | flops 251790592 | bytes 10748544 | tf_op jit(solution)/shard_map/qtm,qtns->mns/dot_general | solution.py:32
  182.8 20.1 %reduce-scatter.7.cloned.1.call-done = bf16[256,128]{1,0:T(8,128)(2,1)} async-done(((bf16[1024,128]{1,0:T(8,128)(2,1)}), bf16[256,128]{1,0:T(8,128)(2,1)}) %reduce-scatter.7.cloned.1.call-update) | async-done | bytes 65552 | tf_op jit(solution)/shard_map/reduce_scatter | solution.py:39
  204.7 31.7 %all_gather.14 = bf16[2048,128]{1,0:T(8,128)(2,1)S(1)} all-gather(bf16[256,128]{1,0:T(8,128)(2,1)S(1)} %fusion.57), channel_id=1, replica_groups=mesh['row'=8,'col'=4] {'row'}, dimensions={0}, use_global_device_ids=true | all-gather | bytes 589824 | tf_op jit(solution)/shard_map/all_gather | solution.py:25
  236.4 12.2 %gather_fusion.2 = bf16[160,128,128]{2,1,0:T(8,128)(2,1)} fusion(bf16[8,2,128,128]{3,2,1,0:T(8,128)(2,1)S(1)} %bitcast.96, s32[160]{0:T(256)S(1)} %reshape.99), kind=kCustom, calls=%fused_computation.2.clone | custom fusion | bytes 10487040 | tf_op jit(solution)/shard_map/jit(take_along_axis)/gather | solution.py:28
  248.5 10.0 %fusion.10 = f32[8,20,128,128]{3,2,1,0:T(8,128)} fusion(bf16[1,1,8,20,128,128]{5,4,3,2,1,0:T(8,128)(2,1)} %param.11, bf16[8,20,128,128]{3,2,1,0:T(8,128)(2,1)} %bitcast.101, pred[8,20]{1,0:T(8,128)(4,1)S(1)} %and_bitcast_fusion), kind=kOutput, calls=%fused_computation.14 | convolution fusion | flops 673710080 | bytes 20971680 | tf_op jit(solution)/shard_map/qtkn,qtks->qtns/dot_general | solution.py:29
  258.6 11.9 %copy.15 = f32[8,20,128,128]{2,1,0,3:T(8,128)} copy(f32[8,20,128,128]{3,2,1,0:T(8,128)} %fusion.10) | data formatting | bytes 20971520 | tf_op jit(solution)/shard_map/qtkn,qtks->qtns/dot_general | solution.py:29
  279.4 20.2 %reduce-scatter.9.cloned.1.call-done = bf16[256,128]{1,0:T(8,128)(2,1)} async-done(((bf16[1024,128]{1,0:T(8,128)(2,1)}), bf16[256,128]{1,0:T(8,128)(2,1)}) %reduce-scatter.9.cloned.1.call-update) | async-done | bytes 65552 | tf_op jit(solution)/shard_map/reduce_scatter | solution.py:39
  301.3 31.9 %all_gather.15 = bf16[2048,128]{1,0:T(8,128)(2,1)S(1)} all-gather(bf16[256,128]{1,0:T(8,128)(2,1)S(1)} %fusion.60), channel_id=1, replica_groups=mesh['row'=8,'col'=4] {'row'}, dimensions={0}, use_global_device_ids=true | all-gather | bytes 589824 | tf_op jit(solution)/shard_map/all_gather | solution.py:25
  333.2 12.2 %gather_fusion.3 = bf16[160,128,128]{2,1,0:T(8,128)(2,1)} fusion(bf16[8,2,128,128]{3,2,1,0:T(8,128)(2,1)S(1)} %bitcast.94, s32[160]{0:T(256)S(1)} %reshape.99), kind=kCustom, calls=%fused_computation.3.clone | custom fusion | bytes 10487040 | tf_op jit(solution)/shard_map/jit(take_along_axis)/gather | solution.py:28
  345.4 10.0 %fusion.8 = f32[8,20,128,128]{3,2,1,0:T(8,128)} fusion(bf16[1,1,8,20,128,128]{5,4,3,2,1,0:T(8,128)(2,1)} %param.11, bf16[8,20,128,128]{3,2,1,0:T(8,128)(2,1)} %bitcast.98, pred[8,20]{1,0:T(8,128)(4,1)S(1)} %and_bitcast_fusion), kind=kOutput, calls=%fused_computation.12 | convolution fusion | flops 673710080 | bytes 20971680 | tf_op jit(solution)/shard_map/qtkn,qtks->qtns/dot_general | solution.py:29
  355.4 11.9 %copy.17 = f32[8,20,128,128]{2,1,0,3:T(8,128)} copy(f32[8,20,128,128]{3,2,1,0:T(8,128)} %fusion.8) | data formatting | bytes 20971520 | tf_op jit(solution)/shard_map/qtkn,qtks->qtns/dot_general | solution.py:29
  367.3 8.1 %fusion.40 = bf16[8,128,128]{2,0,1:T(8,128)(2,1)S(1)} fusion(f32[8,20,128,128]{2,1,0,3:T(8,128)} %copy.17, s32[8,20]{1,0:T(8,128)S(1)} %bitcast.109), kind=kOutput, calls=%fused_computation.36 | convolution fusion | flops 251790592 | bytes 10748544 | tf_op jit(solution)/shard_map/qtm,qtns->mns/dot_general | solution.py:32
  376.2 20.1 %reduce-scatter.11.cloned.1.call-done = bf16[256,128]{1,0:T(8,128)(2,1)} async-done(((bf16[1024,128]{1,0:T(8,128)(2,1)}), bf16[256,128]{1,0:T(8,128)(2,1)}) %reduce-scatter.11.cloned.1.call-update) | async-done | bytes 65552 | tf_op jit(solution)/shard_map/reduce_scatter | solution.py:39
  397.9 39.3 %all-reduce = (f32[128]{0:T(128)S(1)}, f32[128]{0:T(128)S(1)}, f32[128]{0:T(128)S(1)}, f32[128]{0:T(128)S(1)}, f32[128]{0:T(128)S(1)}, /*index=5*/f32[128]{0:T(128)S(1)}, f32[128]{0:T(128)S(1)}, f32[128]{0:T(128)S(1)}) all-reduce(f32[128]{0:T(128)S(1)} %get-tuple-element.10, ...), channel_id=1, replica_groups=mesh['row'=8,'col'=4] {'row','col'}, use_global_device_ids=true, to_apply=%region_5.7 | all-reduce | flops 1024 | bytes 8192 | tf_op jit(solution)/shard_map/psum | solution.py:49
  (40 shorter events, 21.4 us)
Async XLA Ops:
  7.2 99.1 %reduce-scatter.5.cloned.1.call-start = ((), (), s32[]{:S(2)}) async-start(), calls=%async_computation.4 | async-start | bytes 327680 | tf_op jit(solution)/shard_map/reduce_scatter | solution.py:39
  64.1 11.9 %copy-start.5 = (s32[1,1,8,20]{3,2,1,0:T(8,128)S(1)}, s32[1,1,8,20]{3,2,1,0:T(8,128)}, u32[]{:S(2)}) copy-start(s32[1,1,8,20]{3,2,1,0:T(8,128)} %param.10) | copy-start | bytes 1924
  76.0 30.2 %copy-start = (bf16[256,128]{1,0:T(8,128)(2,1)S(1)}, bf16[256,128]{1,0:T(8,128)(2,1)}, u32[]{:S(2)}) copy-start(bf16[256,128]{1,0:T(8,128)(2,1)} %param.7) | copy-start | bytes 196612
  76.0 30.2 %copy-start.4 = (s32[256,128]{1,0:T(8,128)S(1)}, s32[256,128]{1,0:T(8,128)}, u32[]{:S(2)}) copy-start(s32[256,128]{1,0:T(8,128)} %param.8) | copy-start | bytes 393220
  85.0 117.9 %reduce-scatter.7.cloned.1.call-start = ((), (), s32[]{:S(2)}) async-start(), calls=%async_computation.5 | async-start | bytes 327680 | tf_op jit(solution)/shard_map/reduce_scatter | solution.py:39
  182.8 116.8 %reduce-scatter.9.cloned.1.call-start = ((), (), s32[]{:S(2)}) async-start(), calls=%async_computation.6 | async-start | bytes 327680 | tf_op jit(solution)/shard_map/reduce_scatter | solution.py:39
  279.3 117.0 %reduce-scatter.11.cloned.1.call-start = ((), (), s32[]{:S(2)}) async-start(), calls=%async_computation.7 | async-start | bytes 327680 | tf_op jit(solution)/shard_map/reduce_scatter | solution.py:39
  367.3 70.0 %copy-start.1 = (bf16[256,128]{1,0:T(8,128)(2,1)S(1)}, bf16[256,128]{1,0:T(8,128)(2,1)}, u32[]{:S(2)}) copy-start(bf16[256,128]{1,0:T(8,128)(2,1)} %reduce-scatter.5.cloned.1.call-done) | copy-start | bytes 196612
  367.3 70.0 %copy-start.2 = (bf16[256,128]{1,0:T(8,128)(2,1)S(1)}, bf16[256,128]{1,0:T(8,128)(2,1)}, u32[]{:S(2)}) copy-start(bf16[256,128]{1,0:T(8,128)(2,1)} %reduce-scatter.9.cloned.1.call-done) | copy-start | bytes 196612
  367.3 70.0 %copy-start.3 = (bf16[256,128]{1,0:T(8,128)(2,1)S(1)}, bf16[256,128]{1,0:T(8,128)(2,1)}, u32[]{:S(2)}) copy-start(bf16[256,128]{1,0:T(8,128)(2,1)} %reduce-scatter.7.cloned.1.call-done) | copy-start | bytes 196612
Sparse Core Ops, SparseCore 0:
  85.1 21.0 reduce-scatter.4
  182.9 19.9 reduce-scatter.6
  279.4 20.0 reduce-scatter.8
  376.3 19.9 reduce-scatter.10
where the time goes:
time: 455 us; the launch traced here: 446 us
  blocking collectives  168 us (37%)
  local copies, waits for them, and re-layouts  99.3 us (22%)
  waiting for transfers between devices  81.6 us (18%)
  matrix products  72.5 us (16%)
  between operations  14.3 us (3%)
  other arithmetic  10.1 us (2%)
    all_gather x4, blocking collectives, on_device(): gathered = lax.all_gather(current, 'row', axis=0, tiled=True)  129 us
    reduce_scatter x4, waiting for transfers between devices, on_device(): lax.psum_scatter(partial_value.reshape(-1, sources).astype(jnp.bfloat16),...  81.5 us
    gather x5, local copies, waits for them, and re-layouts, on_device(): picked = jnp.take_along_axis(blocked, row_index[:, :, None, None], axis=1)  48.7 us
    dot_general x4, local copies, waits for them, and re-layouts, on_device(): jnp.einsum('qtkn,qtks->qtns', tile_data, picked, preferred_element_type=j...  47.7 us
    dot_general x4, matrix products, on_device(): jnp.einsum('qtkn,qtks->qtns', tile_data, picked, preferred_element_type=j...  40.1 us
    psum x1, blocking collectives, on_device(): counted, totals = lax.psum((counted, totals), ('row', 'col'))  39.3 us
    dot_general x4, matrix products, on_device(): jnp.einsum('qtm,qtns->mns', col_onehot, products, precision=lax.Precision...  32.4 us
  transfers between devices with their start and end apart: 4, of which 4 were waited for; matrix products, arithmetic and copies ran while one was open for 0% of the time, Pallas kernels for 0%

commit v1 on v0

v1 whole, which is shorter than its diff:
```python
import functools

import jax
import jax.numpy as jnp
from jax import lax
from jax.experimental import pallas as pl
from jax.experimental.pallas import tpu as pltpu
from jax.sharding import PartitionSpec as P

LEVELS = 4
HALVES = 1
MESH = pl.DeviceIdType.MESH


def dense_kernel(rows_ref, cols_ref, tiles_ref, out_ref):
    q = pl.program_id(0)
    slots, tile = tiles_ref.shape[1], tiles_ref.shape[-1]
    per_chunk = out_ref.shape[-1] // tile
    out_ref[...] = jnp.zeros_like(out_ref)

    def add(s, carry):
        r = rows_ref[q, s]
        c = cols_ref[q, s]
        at = (
            0,
            c // per_chunk,
            pl.ds(pl.multiple_of(r * tile, tile), tile),
            pl.ds(pl.multiple_of((c % per_chunk) * tile, tile), tile),
        )
        out_ref[at] = out_ref[at] + tiles_ref[0, s]
        return carry

    lax.fori_loop(0, slots, add, 0, unroll=2)


def densify(rows, cols, tiles, n_col, per_dev):
    blocks, slots, tile, unused = tiles.shape
    return pl.pallas_call(
        dense_kernel,
        grid=(blocks,),
        out_shape=jax.ShapeDtypeStruct((blocks, n_col, per_dev, per_dev), jnp.bfloat16),
        in_specs=[
            pl.BlockSpec(memory_space=pltpu.SMEM),
            pl.BlockSpec(memory_space=pltpu.SMEM),
            pl.BlockSpec((1, slots, tile, tile), lambda q: (q, 0, 0, 0)),
        ],
        out_specs=pl.BlockSpec((1, n_col, per_dev, per_dev), lambda q: (q, 0, 0, 0)),
        name="densify",
    )(rows, cols, tiles)


def search_kernel(
    n_row, n_col, n_x, n_core,
    frontier_ref, visited_ref, adj_hbm, depth_out, reach_out,
    adj, cur, acc, part, got, depth_t, held_t, stat_c, stat_r,
    load_sem, ag_send, ag_recv, rs_send, rs_recv, sc_send, sc_recv, sr_send, sr_recv,
):
    n_z = n_row // n_x
    n_y = n_col // n_core
    row, col = lax.axis_index("row"), lax.axis_index("col")
    z, x = row // n_x, row % n_x
    y, core = col // n_core, col % n_core
    halves, width = cur.shape[1], cur.shape[3]

    z_steps = []
    for d in range(1, n_z // 2 + 1):
        z_steps += [d] if d == n_z - d else [d, n_z - d]
    z_peers = [((z + d) % n_z) * n_x + x for d in z_steps]
    x_peers = [z * n_x + (x + d) % n_x for d in range(1, n_x)]
    far_peers = [
        ((z + d) % n_z) * n_x + (x + e) % n_x for d in z_steps for e in range(1, n_x)
    ]
    c_peers = [
        ((y + d) % n_y) * n_core + (core + e) % n_core
        for d in range(1, n_y) for e in range(n_core)
    ] + [y * n_core + (core + e) % n_core for e in range(1, n_core)]
    r_peers = x_peers + z_peers + far_peers

    barrier = pltpu.get_barrier_semaphore()
    for p in r_peers:
        pl.semaphore_signal(barrier, inc=1, device_id=(p, col), device_id_type=MESH)
    for p in c_peers:
        pl.semaphore_signal(barrier, inc=1, device_id=(row, p), device_id_type=MESH)

    loads = [pltpu.make_async_copy(adj_hbm.at[q], adj.at[q], load_sem.at[q]) for q in range(n_row)]
    for load in loads:
        load.start()

    start = frontier_ref[...].astype(jnp.float32).T
    for h in range(halves):
        cur[0, h, row] = start[h * width:(h + 1) * width].astype(jnp.bfloat16)
    seen = (visited_ref[...].T != 0) | (start > 0)
    depth_t[...] = jnp.where(seen, 0, LEVELS + 1)
    held_t[...] = jnp.zeros_like(held_t)

    pl.semaphore_wait(barrier, len(r_peers) + len(c_peers))

    def gather_copy(level, h, q, k, peer):
        par = level % 2
        block = cur.at[level, h, q]
        return pltpu.make_async_remote_copy(
            src_ref=block, dst_ref=block,
            send_sem=ag_send.at[par, h, k], recv_sem=ag_recv.at[par, h, q],
            device_id=(peer, col), device_id_type=MESH,
        )

    def scatter_copy(level, h, d, src_col, peer):
        par = level % 2
        return pltpu.make_async_remote_copy(
            src_ref=part.at[level, h, d], dst_ref=got.at[level, h, src_col],
            send_sem=rs_send.at[par, h, d], recv_sem=rs_recv.at[par, h, src_col],
            device_id=(row, peer), device_id_type=MESH,
        )

    def send_own(level, h):
        for k, p in enumerate(x_peers + z_peers):
            gather_copy(level, h, row, k, p).start()

    for h in range(halves):
        send_own(0, h)
    for load in loads:
        load.wait()

    def multiply(level, h, q, first):
        block = cur[level, h, q]
        for c in range(n_col):
            prod = jnp.dot(block, adj[q, c], preferred_element_type=jnp.float32)
            acc[c] = prod if first else acc[c] + prod

    def one_level(level, carry):
        for h in range(halves):
            k = len(x_peers) + len(z_peers)
            multiply(level, h, row, True)
            for q in z_peers:
                gather_copy(level, h, q, 0, q).wait_recv()
                for p in x_peers:
                    gather_copy(level, h, q, k, p).start()
                    k += 1
                multiply(level, h, q, False)
            tail = x_peers + far_peers
            for q in tail[:-1]:
                gather_copy(level, h, q, 0, q).wait_recv()
                multiply(level, h, q, False)
            last = tail[-1]
            gather_copy(level, h, last, 0, last).wait_recv()
            block = cur[level, h, last]
            for d, p in enumerate(c_peers + [col]):
                total = acc[p] + jnp.dot(block, adj[last, p], preferred_element_type=jnp.float32)
                part[level, h, d] = total.astype(jnp.bfloat16)
                if d < len(c_peers):
                    scatter_copy(level, h, d, col, p).start()
        for h in range(halves):
            here = slice(h * width, (h + 1) * width)
            raw = part[level, h, len(c_peers)].astype(jnp.float32)
            for p in reversed(c_peers):
                scatter_copy(level, h, 0, p, p).wait_recv()
                raw = raw + got[level, h, p].astype(jnp.float32)
            depth = depth_t[here, :]
            fresh = (raw > 0) & (depth == LEVELS + 1)
            held = jnp.where(fresh, raw, 0.0)
            cur[level + 1, h, row] = held.astype(jnp.bfloat16)

            depth_t[here, :] = jnp.where(fresh, level + 1, depth)
            held_t[here, :] = held_t[here, :] + held

            @pl.when(level < LEVELS - 1)
            def _():
                send_own(level + 1, h)
        for h in range(halves):
            for k, p in enumerate(r_peers):
                gather_copy(level, h, row, k, p).wait_send()
            for d, p in enumerate(c_peers):
                scatter_copy(level, h, d, col, p).wait_send()
        return carry

    lax.fori_loop(0, LEVELS, one_level, 0)

    depth = depth_t[...].T
    held = held_t[...].T
    rows = []
    for level in range(1, LEVELS + 1):
        hit = depth == level
        rows.append(jnp.sum(hit.astype(jnp.float32), axis=0, keepdims=True))
        rows.append(jnp.sum(jnp.where(hit, held, 0.0), axis=0, keepdims=True))
    stat_c[col] = jnp.concatenate(rows, axis=0)
    depth_out[...] = depth

    def stat_copy(buf, mine, k, send, recv, device):
        return pltpu.make_async_remote_copy(
            src_ref=buf.at[mine], dst_ref=buf.at[mine],
            send_sem=send.at[k], recv_sem=recv.at[mine],
            device_id=device, device_id_type=MESH,
        )

    def spread(buf, me, peers, send, recv, device):
        for k, p in enumerate(peers):
            stat_copy(buf, me, k, send, recv, device(p)).start()
        total = buf[me]
        for p in peers:
            stat_copy(buf, p, 0, send, recv, device(p)).wait_recv()
            total = total + buf[p]
        for k, p in enumerate(peers):
            stat_copy(buf, me, k, send, recv, device(p)).wait_send()
        return total

    stat_r[row] = spread(stat_c, col, c_peers, sc_send, sc_recv, lambda p: (row, p))
    sums = spread(stat_r, row, r_peers, sr_send, sr_recv, lambda p: (p, col))

    scaling = jnp.ones((1, sums.shape[1]), jnp.float32)
    factor = jnp.zeros_like(held)
    for level in range(1, LEVELS + 1):
        count = sums[2 * level - 2:2 * level - 1]
        total = sums[2 * level - 1:2 * level]
        scaling = scaling / jnp.maximum(scaling * total / jnp.maximum(count, 1.0), 1.0)
        factor = jnp.where(depth == level, scaling, factor)
    reach_out[...] = frontier_ref[...].astype(jnp.float32) + factor * held


def search(frontier, visited, adj, n_row, n_col):
    per_dev, sources = frontier.shape
    n_core = 2 if n_col % 2 == 0 else 1
    n_x = n_col // n_core
    n_x = n_x if n_row % n_x == 0 else 1
    width = sources // HALVES
    dma = pltpu.SemaphoreType.DMA
    vmem = pl.BlockSpec(memory_space=pltpu.VMEM)
    return pl.pallas_call(
        functools.partial(search_kernel, n_row, n_col, n_x, n_core),
        out_shape=(
            jax.ShapeDtypeStruct((per_dev, sources), jnp.int32),
            jax.ShapeDtypeStruct((per_dev, sources), jnp.float32),
        ),
        in_specs=[vmem, vmem, pl.BlockSpec(memory_space=pl.ANY)],
        out_specs=(vmem, vmem),
        scratch_shapes=[
            pltpu.VMEM((n_row, n_col, per_dev, per_dev), jnp.bfloat16),
            pltpu.VMEM((LEVELS + 1, HALVES, n_row, width, per_dev), jnp.bfloat16),
            pltpu.VMEM((n_col, width, per_dev), jnp.float32),
            pltpu.VMEM((LEVELS, HALVES, n_col, width, per_dev), jnp.bfloat16),
            pltpu.VMEM((LEVELS, HALVES, n_col, width, per_dev), jnp.bfloat16),
            pltpu.VMEM((sources, per_dev), jnp.int32),
            pltpu.VMEM((sources, per_dev), jnp.float32),
            pltpu.VMEM((n_col, 2 * LEVELS, sources), jnp.float32),
            pltpu.VMEM((n_row, 2 * LEVELS, sources), jnp.float32),
            dma((n_row,)),
            dma((2, HALVES, n_row)),
            dma((2, HALVES, n_row)),
            dma((2, HALVES, n_col)),
            dma((2, HALVES, n_col)),
            dma((n_col,)),
            dma((n_col,)),
            dma((n_row,)),
            dma((n_row,)),
        ],
        compiler_params=pltpu.CompilerParams(
            collective_id=0, has_side_effects=True, vmem_limit_bytes=60 * 1024 * 1024
        ),
        name="search",
    )(frontier, visited, adj)


def solution(mesh):
    n_row, n_col = mesh.shape["row"], mesh.shape["col"]

    def on_device(frontier, visited, tile_rows, tile_cols, tile_bits):
        per_dev = frontier.shape[0]
        adj = densify(tile_rows[0, 0], tile_cols[0, 0], tile_bits[0, 0], n_col, per_dev)
        return search(frontier, visited, adj, n_row, n_col)

    placed = (
        P(("row", "col"), None),
        P(("row", "col"), None),
        P("row", "col", None, None),
        P("row", "col", None, None),
        P("row", "col", None, None, None, None),
    )
    return jax.shard_map(
        on_device,
        mesh=mesh,
        in_specs=placed,
        out_specs=(P(("row", "col"), None), P(("row", "col"), None)),
        check_vma=False,
    )
```

time: 455 us -> 87.1 us (0.19); the launches traced: 446 us -> 86.8 us
  blocking collectives: 168 us -> 0 us
  local copies, waits for them, and re-layouts: 99.3 us -> 3.14 us
  Pallas kernels: 0 us -> 83 us
  waiting for transfers between devices: 81.6 us -> 0 us
  matrix products: 72.5 us -> 0 us
  between operations: 14.3 us -> 0.64 us
  other arithmetic: 10.1 us -> 0 us
    all_gather x4 -> x0, blocking collectives: 129 us -> none  [on_device(): gathered = lax.all_gather(current, 'row', axis=0, tiled=True)]
    pallas_call x0 -> x2, Pallas kernels: none -> 83 us  [the longest x1 75 us: search(): pl.pallas_call(functools.partial(search_kernel, n_row, n_col, n_x, n_core...]
    reduce_scatter x4 -> x0, waiting for transfers between devices: 81.5 us -> none  [on_device(): lax.psum_scatter(partial_value.reshape(-1, sources).astype(jnp.bfloat16),...]
    dot_general x8 -> x0, matrix products: 72.5 us -> none  [the longest x4 40.1 us: on_device(): jnp.einsum('qtkn,qtks->qtns', tile_data, picked, preferred_element_type=j...]
    gather x5 -> x0, local copies, waits for them, and re-layouts: 48.7 us -> none  [on_device(): picked = jnp.take_along_axis(blocked, row_index[:, :, None, None], axis=1)]
    dot_general x4 -> x0, local copies, waits for them, and re-layouts: 47.7 us -> none  [on_device(): jnp.einsum('qtkn,qtks->qtns', tile_data, picked, preferred_element_type=j...]
    psum x1 -> x0, blocking collectives: 39.3 us -> none  [on_device(): counted, totals = lax.psum((counted, totals), ('row', 'col'))]
  transfers between devices with their start and end apart: 4 -> 0, of which waited for: 4 -> 0; matrix products, arithmetic and copies ran while one was open for 0% -> 0% of each run, Pallas kernels for 0% -> 0%
where the time goes in v1:
time: 87.1 us; the launch traced here: 86.8 us
  Pallas kernels  83 us (95%)
  local copies, waits for them, and re-layouts  3.14 us (4%)
    pallas_call x1, Pallas kernels, search(): pl.pallas_call(functools.partial(search_kernel, n_row, n_col, n_x, n_core...  75 us
    pallas_call x1, Pallas kernels, densify(): pl.pallas_call(dense_kernel, grid=(blocks,), out_shape=jax.ShapeDtypeStru...  8.02 us
    unnamed x2, local copies, waits for them, and re-layouts  3.14 us

profile of v1, /device:TPU:0, one launch (start us, length us, event | category | flops | bytes accessed | tf_op | source)
XLA Modules:
  0.0 86.8 jit_solution(10969091453390126068)
XLA Ops:
  0.6 8.0 %densify.1.adj_hbm = bf16[8,4,256,256]{3,2,1,0:T(8,128)(2,1)} custom-call(s32[8,20]{1,0:T(8,128)} %bitcast.4, s32[8,20]{1,0:T(8,128)} %bitcast.5, bf16[8,20,128,128]{3,2,1,0:T(8,128)(2,1)} %bitcast.3), custom_call_target="tpu_custom_call" | custom-call | tf_op jit(solution)/shard_map/densify/pallas_call | solution.py:38
  8.7 75.0 %search.1 = (s32[256,128]{1,0:T(8,128)}, f32[256,128]{1,0:T(8,128)}) custom-call(bf16[256,128]{1,0:T(8,128)(2,1)} %frontier_ref.1, s32[256,128]{1,0:T(8,128)} %visited_ref.1, bf16[8,4,256,256]{3,2,1,0:T(8,128)(2,1)} %densify.1.adj_hbm), custom_call_target="tpu_custom_call" | custom-call | tf_op jit(solution)/shard_map/search/pallas_call | solution.py:227
  83.7 1.6 %copy.9 = s32[256,128]{1,0:T(8,128)} copy(s32[256,128]{1,0:T(8,128)} %get-tuple-element.4) | data formatting | bytes 262144
  85.2 1.6 %copy.10 = f32[256,128]{1,0:T(8,128)} copy(f32[256,128]{1,0:T(8,128)} %get-tuple-element.5) | data formatting | bytes 262144

commit v2 on v1

v2 whole, which is shorter than its diff:
```python
import functools

import jax
import jax.numpy as jnp
from jax import lax
from jax.experimental import pallas as pl
from jax.experimental.pallas import tpu as pltpu
from jax.sharding import PartitionSpec as P

LEVELS = 4
HALVES = 2
MESH = pl.DeviceIdType.MESH


def search_kernel(
    n_row, n_col, n_x, n_core,
    frontier_ref, visited_ref, rows_ref, cols_ref, tiles_hbm, depth_out, reach_out,
    tiles, key_v, prev_v, last_v, prev_s, last_s, adj, cur, acc, part, got, depth_t, held_t, stat_c, stat_r,
    load_sem, index_sem, ag_send, ag_recv, rs_send, rs_recv, sc_send, sc_recv, sr_send, sr_recv,
):
    n_z = n_row // n_x
    n_y = n_col // n_core
    row, col = lax.axis_index("row"), lax.axis_index("col")
    z, x = row // n_x, row % n_x
    y, core = col // n_core, col % n_core
    halves, width = cur.shape[1], cur.shape[3]

    z_steps = []
    for d in range(1, n_z // 2 + 1):
        z_steps += [d] if d == n_z - d else [d, n_z - d]
    z_peers = [((z + d) % n_z) * n_x + x for d in z_steps]
    x_peers = [z * n_x + (x + d) % n_x for d in range(1, n_x)]
    far_peers = [
        ((z + d) % n_z) * n_x + (x + e) % n_x for d in z_steps for e in range(1, n_x)
    ]
    c_peers = [
        ((y + d) % n_y) * n_core + (core + e) % n_core
        for d in range(1, n_y) for e in range(n_core)
    ] + [y * n_core + (core + e) % n_core for e in range(1, n_core)]
    r_peers = x_peers + z_peers + far_peers

    barrier = pltpu.get_barrier_semaphore()
    for p in r_peers:
        pl.semaphore_signal(barrier, inc=1, device_id=(p, col), device_id_type=MESH)
    for p in c_peers:
        pl.semaphore_signal(barrier, inc=1, device_id=(row, p), device_id_type=MESH)

    slots, tile = tiles_hbm.shape[1], tiles_hbm.shape[-1]
    per_chunk = adj.shape[-1] // tile
    loads = [
        pltpu.make_async_copy(tiles_hbm.at[q], tiles.at[q, pl.ds(0, slots)], load_sem.at[q])
        for q in range(n_row)
    ]
    for load in loads:
        load.start()

    key_v[...] = jnp.full_like(key_v, -1)
    key_v[:, pl.ds(0, slots)] = rows_ref[...] * (n_col * per_chunk) + cols_ref[...]
    key = key_v[...]
    lane = lax.broadcasted_iota(jnp.int32, key.shape, 1)
    prev = jnp.full(key.shape, slots, jnp.int32)
    last = jnp.full(key.shape, slots, jnp.int32)
    for t in range(slots):
        this = key[:, t:t + 1]
        prev = jnp.where((this == key) & (lane > t), t, prev)
        last = jnp.where(this == lane, t, last)
    prev_v[...] = prev
    last_v[...] = last
    tables = [
        pltpu.make_async_copy(prev_v, prev_s, index_sem.at[0]),
        pltpu.make_async_copy(last_v, last_s, index_sem.at[1]),
    ]
    for table in tables:
        table.start()
    for q in range(n_row):
        tiles[q, slots] = jnp.zeros((tile, tile), jnp.bfloat16)

    start = frontier_ref[...].astype(jnp.float32).T
    for h in range(halves):
        cur[0, h, row] = start[h * width:(h + 1) * width].astype(jnp.bfloat16)
    seen = (visited_ref[...].T != 0) | (start > 0)
    depth_t[...] = jnp.where(seen, 0, LEVELS + 1)
    held_t[...] = jnp.zeros_like(held_t)

    for table in tables:
        table.wait()
    for load in loads:
        load.wait()

    def chain(s, carry):
        for q in range(0, n_row, 4):
            group = range(q, min(q + 4, n_row))
            sums = [tiles[g, s] + tiles[g, prev_s[g, s]] for g in group]
            for g, total in zip(group, sums):
                tiles[g, s] = total
        return carry

    lax.fori_loop(1, slots, chain, 0)

    def place(q, carry):
        for r in range(adj.shape[2] // tile):
            for c in range(n_col * per_chunk):
                low = (c % per_chunk) * tile
                adj[q, c // per_chunk, r * tile:(r + 1) * tile, low:low + tile] = (
                    tiles[q, last_s[q, r * n_col * per_chunk + c]]
                )
        return carry

    pl.semaphore_wait(barrier, len(r_peers) + len(c_peers))

    def gather_copy(level, h, q, k, peer):
        par = level % 2
        block = cur.at[level, h, q]
        return pltpu.make_async_remote_copy(
            src_ref=block, dst_ref=block,
            send_sem=ag_send.at[par, h, k], recv_sem=ag_recv.at[par, h, q],
            device_id=(peer, col), device_id_type=MESH,
        )

    def scatter_copy(level, h, d, src_col, peer):
        par = level % 2
        return pltpu.make_async_remote_copy(
            src_ref=part.at[level, h, d], dst_ref=got.at[level, h, src_col],
            send_sem=rs_send.at[par, h, d], recv_sem=rs_recv.at[par, h, src_col],
            device_id=(row, peer), device_id_type=MESH,
        )

    def send_own(level, h):
        for k, p in enumerate(x_peers + z_peers):
            gather_copy(level, h, row, k, p).start()

    for h in range(halves):
        send_own(0, h)
    lax.fori_loop(0, n_row, place, 0)

    def multiply(level, h, q, first):
        block = cur[level, h, q]
        for c in range(n_col):
            prod = jnp.dot(block, adj[q, c], preferred_element_type=jnp.float32)
            acc[h, c] = prod if first else acc[h, c] + prod

    def take_z(level, h):
        k = len(x_peers) + len(z_peers)
        multiply(level, h, row, True)
        for q in z_peers:
            gather_copy(level, h, q, 0, q).wait_recv()
            for p in x_peers:
                gather_copy(level, h, q, k, p).start()
                k += 1
            multiply(level, h, q, False)

    def take_x(level, h):
        tail = x_peers + far_peers
        for q in tail[:-1]:
            gather_copy(level, h, q, 0, q).wait_recv()
            multiply(level, h, q, False)
        last = tail[-1]
        gather_copy(level, h, last, 0, last).wait_recv()
        block = cur[level, h, last]
        for d, p in enumerate(c_peers + [col]):
            total = acc[h, p] + jnp.dot(block, adj[last, p], preferred_element_type=jnp.float32)
            part[level, h, d] = total.astype(jnp.bfloat16)
            if d < len(c_peers):
                scatter_copy(level, h, d, col, p).start()

    def close(level, h):
        here = slice(h * width, (h + 1) * width)
        raw = part[level, h, len(c_peers)].astype(jnp.float32)
        for p in reversed(c_peers):
            scatter_copy(level, h, 0, p, p).wait_recv()
            raw = raw + got[level, h, p].astype(jnp.float32)
        depth = depth_t[here, :]
        fresh = (raw > 0) & (depth == LEVELS + 1)
        held = jnp.where(fresh, raw, 0.0)
        cur[level + 1, h, row] = held.astype(jnp.bfloat16)
        depth_t[here, :] = jnp.where(fresh, level + 1, depth)
        held_t[here, :] = held_t[here, :] + held

        @pl.when(level < LEVELS - 1)
        def _():
            send_own(level + 1, h)

        for k, p in enumerate(r_peers):
            gather_copy(level, h, row, k, p).wait_send()
        for d, p in enumerate(c_peers):
            scatter_copy(level, h, d, col, p).wait_send()

    def one_level(level, carry):
        for h in range(halves - 1):
            take_x(level, h)
        take_z(level, halves - 1)
        for h in range(halves - 1):
            close(level, h)
        take_x(level, halves - 1)

        @pl.when(level < LEVELS - 1)
        def _():
            for h in range(halves - 1):
                take_z(level + 1, h)

        close(level, halves - 1)
        return carry

    for h in range(halves - 1):
        take_z(0, h)
    lax.fori_loop(0, LEVELS, one_level, 0)

    depth = depth_t[...].T
    held = held_t[...].T
    rows = []
    for level in range(1, LEVELS + 1):
        hit = depth == level
        rows.append(jnp.sum(hit.astype(jnp.float32), axis=0, keepdims=True))
        rows.append(jnp.sum(jnp.where(hit, held, 0.0), axis=0, keepdims=True))
    stat_c[col] = jnp.concatenate(rows, axis=0)
    depth_out[...] = depth

    def stat_copy(buf, mine, k, send, recv, device):
        return pltpu.make_async_remote_copy(
            src_ref=buf.at[mine], dst_ref=buf.at[mine],
            send_sem=send.at[k], recv_sem=recv.at[mine],
            device_id=device, device_id_type=MESH,
        )

    def spread(buf, me, peers, send, recv, device):
        for k, p in enumerate(peers):
            stat_copy(buf, me, k, send, recv, device(p)).start()
        total = buf[me]
        for p in peers:
            stat_copy(buf, p, 0, send, recv, device(p)).wait_recv()
            total = total + buf[p]
        for k, p in enumerate(peers):
            stat_copy(buf, me, k, send, recv, device(p)).wait_send()
        return total

    stat_r[row] = spread(stat_c, col, c_peers, sc_send, sc_recv, lambda p: (row, p))
    sums = spread(stat_r, row, r_peers, sr_send, sr_recv, lambda p: (p, col))

    scaling = jnp.ones((1, sums.shape[1]), jnp.float32)
    factor = jnp.zeros_like(held)
    for level in range(1, LEVELS + 1):
        count = sums[2 * level - 2:2 * level - 1]
        total = sums[2 * level - 1:2 * level]
        scaling = scaling / jnp.maximum(scaling * total / jnp.maximum(count, 1.0), 1.0)
        factor = jnp.where(depth == level, scaling, factor)
    reach_out[...] = frontier_ref[...].astype(jnp.float32) + factor * held


def search(frontier, visited, rows, cols, tiles, n_row, n_col):
    blocks, slots, tile, unused = tiles.shape
    per_dev, sources = frontier.shape
    places = (per_dev // tile) * (n_col * per_dev // tile)
    table = (blocks, 128 * (max(slots, places) // 128 + 1))
    n_core = 2 if n_col % 2 == 0 else 1
    n_x = n_col // n_core
    n_x = n_x if n_row % n_x == 0 else 1
    width = sources // HALVES
    dma = pltpu.SemaphoreType.DMA
    vmem = pl.BlockSpec(memory_space=pltpu.VMEM)
    return pl.pallas_call(
        functools.partial(search_kernel, n_row, n_col, n_x, n_core),
        out_shape=(
            jax.ShapeDtypeStruct((per_dev, sources), jnp.int32),
            jax.ShapeDtypeStruct((per_dev, sources), jnp.float32),
        ),
        in_specs=[vmem, vmem, vmem, vmem, pl.BlockSpec(memory_space=pl.ANY)],
        out_specs=(vmem, vmem),
        scratch_shapes=[
            pltpu.VMEM((blocks, slots + 1, tile, tile), jnp.bfloat16),
            pltpu.VMEM(table, jnp.int32),
            pltpu.VMEM(table, jnp.int32),
            pltpu.VMEM(table, jnp.int32),
            pltpu.SMEM(table, jnp.int32),
            pltpu.SMEM(table, jnp.int32),
            pltpu.VMEM((n_row, n_col, per_dev, per_dev), jnp.bfloat16),
            pltpu.VMEM((LEVELS + 1, HALVES, n_row, width, per_dev), jnp.bfloat16),
            pltpu.VMEM((HALVES, n_col, width, per_dev), jnp.float32),
            pltpu.VMEM((LEVELS, HALVES, n_col, width, per_dev), jnp.bfloat16),
            pltpu.VMEM((LEVELS, HALVES, n_col, width, per_dev), jnp.bfloat16),
            pltpu.VMEM((sources, per_dev), jnp.int32),
            pltpu.VMEM((sources, per_dev), jnp.float32),
            pltpu.VMEM((n_col, 2 * LEVELS, sources), jnp.float32),
            pltpu.VMEM((n_row, 2 * LEVELS, sources), jnp.float32),
            dma((n_row,)),
            dma((2,)),
            dma((2, HALVES, n_row)),
            dma((2, HALVES, n_row)),
            dma((2, HALVES, n_col)),
            dma((2, HALVES, n_col)),
            dma((n_col,)),
            dma((n_col,)),
            dma((n_row,)),
            dma((n_row,)),
        ],
        compiler_params=pltpu.CompilerParams(
            collective_id=0, has_side_effects=True, vmem_limit_bytes=60 * 1024 * 1024
        ),
        name="search",
    )(frontier, visited, rows, cols, tiles)


def solution(mesh):
    n_row, n_col = mesh.shape["row"], mesh.shape["col"]

    def on_device(frontier, visited, tile_rows, tile_cols, tile_bits):
        return search(
            frontier, visited, tile_rows[0, 0], tile_cols[0, 0], tile_bits[0, 0], n_row, n_col
        )

    placed = (
        P(("row", "col"), None),
        P(("row", "col"), None),
        P("row", "col", None, None),
        P("row", "col", None, None),
        P("row", "col", None, None, None, None),
    )
    return jax.shard_map(
        on_device,
        mesh=mesh,
        in_specs=placed,
        out_specs=(P(("row", "col"), None), P(("row", "col"), None)),
        check_vma=False,
    )
```

time: 87.1 us -> 73.7 us (0.85)
  Pallas kernels: 83 us -> 69.8 us
    pallas_call x1 -> x0, Pallas kernels: 8.02 us -> none  [densify(): pl.pallas_call(dense_kernel, grid=(blocks,), out_shape=jax.ShapeDtypeStru...]
    pallas_call x1, Pallas kernels: 75 us -> 69.8 us  [search(): pl.pallas_call(functools.partial(search_kernel, n_row, n_col, n_x, n_core...]
where the time goes in v2:
time: 73.7 us; the launch traced here: 73.5 us
  Pallas kernels  69.8 us (95%)
  local copies, waits for them, and re-layouts  3.14 us (4%)
    pallas_call x1, Pallas kernels, search(): pl.pallas_call(functools.partial(search_kernel, n_row, n_col, n_x, n_core...  69.8 us
    unnamed x2, local copies, waits for them, and re-layouts  3.14 us

profile of v2, /device:TPU:0, one launch (start us, length us, event | category | flops | bytes accessed | tf_op | source)
XLA Modules:
  0.0 73.5 jit_solution(170474622585433685)
XLA Ops:
  0.6 69.8 %search.1 = (s32[256,128]{1,0:T(8,128)}, f32[256,128]{1,0:T(8,128)}) custom-call(bf16[256,128]{1,0:T(8,128)(2,1)} %frontier_ref.1, s32[256,128]{1,0:T(8,128)} %visited_ref.1, s32[8,20]{1,0:T(8,128)} %bitcast.4, s32[8,20]{1,0:T(8,128)} %bitcast.5, bf16[8,20,128,128]{3,2,1,0:T(8,128)(2,1)} %bitcast.3), custom_call_target="tpu_custom_call" | custom-call | tf_op jit(solution)/shard_map/search/pallas_call | solution.py:260
  70.4 1.6 %copy.9 = s32[256,128]{1,0:T(8,128)} copy(s32[256,128]{1,0:T(8,128)} %get-tuple-element.4) | data formatting | bytes 262144
  72.0 1.6 %copy.10 = f32[256,128]{1,0:T(8,128)} copy(f32[256,128]{1,0:T(8,128)} %get-tuple-element.5) | data formatting | bytes 262144

commit v3 on v2

--- a/solution.py
+++ b/solution.py
@@ -17,6 +17,7 @@
     frontier_ref, visited_ref, rows_ref, cols_ref, tiles_hbm, depth_out, reach_out,
     tiles, key_v, prev_v, last_v, prev_s, last_s, adj, cur, acc, part, got, depth_t, held_t, stat_c, stat_r,
     load_sem, index_sem, ag_send, ag_recv, rs_send, rs_recv, sc_send, sc_recv, sr_send, sr_recv,
+    stat_f, sf_sem,
 ):
     n_z = n_row // n_x
     n_y = n_col // n_core
@@ -25,13 +26,17 @@
     y, core = col // n_core, col % n_core
     halves, width = cur.shape[1], cur.shape[3]
 
-    z_steps = []
-    for d in range(1, n_z // 2 + 1):
-        z_steps += [d] if d == n_z - d else [d, n_z - d]
-    z_peers = [((z + d) % n_z) * n_x + x for d in z_steps]
+    side = z // max(n_z // 2, 1) if n_z % 2 == 0 else 0
+    near = z + side * (n_z - 1 - 2 * z)
+    z_rows = []
+    for k in range(n_z - 1):
+        t = n_z - 1 - k
+        t = t - (near - t + n_z) // n_z
+        z_rows.append(t + side * (n_z - 1 - 2 * t))
+    z_peers = [t * n_x + x for t in z_rows]
     x_peers = [z * n_x + (x + d) % n_x for d in range(1, n_x)]
     far_peers = [
-        ((z + d) % n_z) * n_x + (x + e) % n_x for d in z_steps for e in range(1, n_x)
+        t * n_x + (x + e) % n_x for t in reversed(z_rows) for e in range(1, n_x)
     ]
     c_peers = [
         ((y + d) % n_y) * n_core + (core + e) % n_core
@@ -39,11 +44,20 @@
     ] + [y * n_core + (core + e) % n_core for e in range(1, n_core)]
     r_peers = x_peers + z_peers + far_peers
 
+    n_all = n_row * n_col
+    me = row * n_col + col
+
+    def device(k):
+        p = (me + k) % n_all
+        return (p // n_col, p % n_col)
+
     barrier = pltpu.get_barrier_semaphore()
-    for p in r_peers:
-        pl.semaphore_signal(barrier, inc=1, device_id=(p, col), device_id_type=MESH)
-    for p in c_peers:
-        pl.semaphore_signal(barrier, inc=1, device_id=(row, p), device_id_type=MESH)
+
+    def greet(k, carry):
+        pl.semaphore_signal(barrier, inc=1, device_id=device(k), device_id_type=MESH)
+        return carry
+
+    lax.fori_loop(1, n_all, greet, 0)
 
     slots, tile = tiles_hbm.shape[1], tiles_hbm.shape[-1]
     per_chunk = adj.shape[-1] // tile
@@ -95,7 +109,6 @@
                 tiles[g, s] = total
         return carry
 
-    lax.fori_loop(1, slots, chain, 0)
 
     def place(q, carry):
         for r in range(adj.shape[2] // tile):
@@ -106,7 +119,6 @@
                 )
         return carry
 
-    pl.semaphore_wait(barrier, len(r_peers) + len(c_peers))
 
     def gather_copy(level, h, q, k, peer):
         par = level % 2
@@ -129,8 +141,10 @@
         for k, p in enumerate(x_peers + z_peers):
             gather_copy(level, h, row, k, p).start()
 
+    pl.semaphore_wait(barrier, n_all - 1)
     for h in range(halves):
         send_own(0, h)
+    lax.fori_loop(1, slots, chain, 0)
     lax.fori_loop(0, n_row, place, 0)
 
     def multiply(level, h, q, first):
@@ -142,7 +156,7 @@
     def take_z(level, h):
         k = len(x_peers) + len(z_peers)
         multiply(level, h, row, True)
-        for q in z_peers:
+        for q in reversed(z_peers):
             gather_copy(level, h, q, 0, q).wait_recv()
             for p in x_peers:
                 gather_copy(level, h, q, k, p).start()
@@ -185,10 +199,49 @@
         for d, p in enumerate(c_peers):
             scatter_copy(level, h, d, col, p).wait_send()
 
+    def stat_rows(depth, held, levels):
+        rows = []
+        for level in levels:
+            hit = depth == level
+            rows.append(jnp.sum(hit.astype(jnp.float32), axis=0, keepdims=True))
+            rows.append(jnp.sum(jnp.where(hit, held, 0.0), axis=0, keepdims=True))
+        return jnp.concatenate(rows, axis=0)
+
+    def stat_copy(buf, mine, k, send, recv, peer):
+        return pltpu.make_async_remote_copy(
+            src_ref=buf.at[mine], dst_ref=buf.at[mine],
+            send_sem=send.at[k], recv_sem=recv.at[mine],
+            device_id=peer, device_id_type=MESH,
+        )
+
+    def spread(buf, mine, peers, send, recv, place_of):
+        for k, p in enumerate(peers):
+            stat_copy(buf, mine, k, send, recv, place_of(p)).start()
+
+    def collect(buf, mine, peers, send, recv, place_of):
+        total = buf[mine]
+        for p in peers:
+            stat_copy(buf, p, 0, send, recv, place_of(p)).wait_recv()
+            total = total + buf[p]
+        for k, p in enumerate(peers):
+            stat_copy(buf, mine, k, send, recv, place_of(p)).wait_send()
+        return total
+
+    over_col = (stat_c, col, c_peers, sc_send, sc_recv, lambda p: (row, p))
+    over_row = (stat_r, row, r_peers, sr_send, sr_recv, lambda p: (p, col))
+
     def one_level(level, carry):
         for h in range(halves - 1):
             take_x(level, h)
         take_z(level, halves - 1)
+
+        @pl.when(level == LEVELS - 1)
+        def _():
+            rows = stat_rows(depth_t[...].T, held_t[...].T, range(1, LEVELS))
+            stat_c[col, pl.ds(0, 2 * LEVELS - 2)] = rows
+            stat_c[col, pl.ds(2 * LEVELS - 2, 2)] = jnp.zeros((2, rows.shape[1]), jnp.float32)
+            spread(*over_col)
+
         for h in range(halves - 1):
             close(level, h)
         take_x(level, halves - 1)
@@ -198,6 +251,11 @@
             for h in range(halves - 1):
                 take_z(level + 1, h)
 
+        @pl.when(level == LEVELS - 1)
+        def _():
+            stat_r[row] = collect(*over_col)
+            spread(*over_row)
+
         close(level, halves - 1)
         return carry
 
@@ -207,34 +265,25 @@
 
     depth = depth_t[...].T
     held = held_t[...].T
-    rows = []
-    for level in range(1, LEVELS + 1):
-        hit = depth == level
-        rows.append(jnp.sum(hit.astype(jnp.float32), axis=0, keepdims=True))
-        rows.append(jnp.sum(jnp.where(hit, held, 0.0), axis=0, keepdims=True))
-    stat_c[col] = jnp.concatenate(rows, axis=0)
+    stat_f[me] = stat_rows(depth, held, [LEVELS])
+
+    def final_copy(part_ref, peer):
+        return pltpu.make_async_remote_copy(
+            src_ref=part_ref, dst_ref=part_ref, send_sem=sf_sem.at[0], recv_sem=sf_sem.at[1],
+            device_id=peer, device_id_type=MESH,
+        )
+
+    def tell(k, carry):
+        final_copy(stat_f.at[me], device(k)).start()
+        return carry
+
+    lax.fori_loop(1, n_all, tell, 0)
     depth_out[...] = depth
-
-    def stat_copy(buf, mine, k, send, recv, device):
-        return pltpu.make_async_remote_copy(
-            src_ref=buf.at[mine], dst_ref=buf.at[mine],
-            send_sem=send.at[k], recv_sem=recv.at[mine],
-            device_id=device, device_id_type=MESH,
-        )
-
-    def spread(buf, me, peers, send, recv, device):
-        for k, p in enumerate(peers):
-            stat_copy(buf, me, k, send, recv, device(p)).start()
-        total = buf[me]
-        for p in peers:
-            stat_copy(buf, p, 0, send, recv, device(p)).wait_recv()
-            total = total + buf[p]
-        for k, p in enumerate(peers):
-            stat_copy(buf, me, k, send, recv, device(p)).wait_send()
-        return total
-
-    stat_r[row] = spread(stat_c, col, c_peers, sc_send, sc_recv, lambda p: (row, p))
-    sums = spread(stat_r, row, r_peers, sr_send, sr_recv, lambda p: (p, col))
+    sums = collect(*over_row)
+    others = final_copy(stat_f.at[pl.ds(0, n_all - 1)], device(1))
+    others.wait_recv()
+    others.wait_send()
+    sums = jnp.concatenate([sums[:2 * LEVELS - 2], jnp.sum(stat_f[...], axis=0)], axis=0)
 
     scaling = jnp.ones((1, sums.shape[1]), jnp.float32)
     factor = jnp.zeros_like(held)
@@ -291,6 +340,8 @@
             dma((n_col,)),
             dma((n_row,)),
             dma((n_row,)),
+            pltpu.VMEM((n_row * n_col, 2, sources), jnp.float32),
+            dma((2,)),
         ],
         compiler_params=pltpu.CompilerParams(
             collective_id=0, has_side_effects=True, vmem_limit_bytes=60 * 1024 * 1024

time: 73.7 us -> 71.1 us (0.965)
  Pallas kernels: 69.8 us -> 67.1 us
    pallas_call x1, Pallas kernels: 69.8 us -> 67.1 us  [search(): pl.pallas_call(functools.partial(search_kernel, n_row, n_col, n_x, n_core...]
where the time goes in v3:
time: 71.1 us; the launch traced here: 70.9 us
  Pallas kernels  67.1 us (94%)
  local copies, waits for them, and re-layouts  3.14 us (4%)
    pallas_call x1, Pallas kernels, search(): pl.pallas_call(functools.partial(search_kernel, n_row, n_col, n_x, n_core...  67.1 us
    unnamed x2, local copies, waits for them, and re-layouts  3.14 us

profile of v3, /device:TPU:0, one launch (start us, length us, event | category | flops | bytes accessed | tf_op | source)
XLA Modules:
  0.0 70.9 jit_solution(16595685453388025603)
XLA Ops:
  0.6 67.1 %search.1 = (s32[256,128]{1,0:T(8,128)}, f32[256,128]{1,0:T(8,128)}) custom-call(bf16[256,128]{1,0:T(8,128)(2,1)} %frontier_ref.1, s32[256,128]{1,0:T(8,128)} %visited_ref.1, s32[8,20]{1,0:T(8,128)} %bitcast.4, s32[8,20]{1,0:T(8,128)} %bitcast.5, bf16[8,20,128,128]{3,2,1,0:T(8,128)(2,1)} %bitcast.3), custom_call_target="tpu_custom_call" | custom-call | tf_op jit(solution)/shard_map/search/pallas_call | solution.py:309
  67.7 1.6 %copy.9 = s32[256,128]{1,0:T(8,128)} copy(s32[256,128]{1,0:T(8,128)} %get-tuple-element.4) | data formatting | bytes 262144
  69.3 1.6 %copy.10 = f32[256,128]{1,0:T(8,128)} copy(f32[256,128]{1,0:T(8,128)} %get-tuple-element.5) | data formatting | bytes 262144
